TPU v7x, 32 devices: a whole 2x2x4 slice. The times are simulated.
32 devices in a mesh: grp: 4 (over z), dev: 8 (over y, x, core).
Axes of the slice: x: 2, y: 2, z: 4, core: 2. Of those that a mesh axis runs over, the one named last changes fastest.
Arguments:
- matrix_tiles: bfloat16 [640, 128, 1024], P(('grp', 'dev')), may hold values from -0.125 to 0.125
- tile_column: int32 [640], P(('grp', 'dev')), may hold values from 0 to 255
- block_counts: int32 [256], P(('grp', 'dev')), may hold values from 1 to 4, as said below
- destination: int32 [256], P(('grp', 'dev')), may hold values from 0 to 7, as said below
- row_bounds: bfloat16 [32768], P(('grp', 'dev')), may hold values from -6 to 6
- dual_start: bfloat16 [32768], P(('grp', 'dev')), may hold values from 0 to 1
- primal_start: float32 [262144], replicated, may hold values from 0 to 0.5
- cost_vector: float32 [262144], replicated, may hold values from -6 to 6
- upper_bound: float32 [262144], replicated, may hold values from 0.5 to 2
Outputs:
- primal_final: float32 [262144], replicated
- dual_final: float32 [32768], P(('grp', 'dev'))
- weight_final: float32 [1], replicated
Inputs may be any that keep to these rules, and one draw needn't show every extreme that they name: `block_counts`: each device's 8 row blocks have 1 to 4 tiles each and 20 at most together; some device has exactly 20 in every draw. `destination`: on every device the 8 entries are each of 0 to 7 once.
All inputs are finite; a program needn't handle non-finite values.
Results may differ from a plain program's by a relative error of at most 0.0015.
Values may be sent and summed in bfloat16 or wider, within the bound.
A program may use at most 128 MiB of HBM per device.

v0:
```python
import jax
import jax.numpy as jnp
from jax import lax
from jax.sharding import PartitionSpec as P

NCB = 256
ITERS = 3
step_scale = 0.3


def row_products(tile_store, vector_bf, blocks):
    tile_set, tile_cols, owners, live_flags = tile_store
    vector_table = vector_bf.reshape(-1, tile_set.shape[2])
    column_hot = (
        tile_cols[:, None] == jnp.arange(vector_table.shape[0], dtype=jnp.int32)[None, :]
    ).astype(jnp.bfloat16)
    picked = jnp.dot(column_hot, vector_table, preferred_element_type=jnp.float32).astype(
        jnp.bfloat16
    )
    product = jnp.einsum("src,sc->sr", tile_set, picked, preferred_element_type=jnp.float32)
    product = jnp.where(live_flags[:, None], product, 0.0)
    owner_hot = (jnp.arange(blocks, dtype=jnp.int32)[:, None] == owners[None, :]).astype(
        jnp.float32
    )
    return jnp.dot(owner_hot, product, precision=lax.Precision.HIGHEST)


def column_products(tile_store, rows_bf):
    tile_set, tile_cols, owners, live_flags = tile_store
    blocks = rows_bf.shape[0]
    owner_hot = (owners[:, None] == jnp.arange(blocks, dtype=jnp.int32)[None, :]).astype(
        jnp.bfloat16
    )
    picked_rows = jnp.dot(owner_hot, rows_bf, preferred_element_type=jnp.float32).astype(
        jnp.bfloat16
    )
    product = jnp.einsum("src,sr->sc", tile_set, picked_rows, preferred_element_type=jnp.float32)
    product = jnp.where(live_flags[:, None], product, 0.0)
    column_hot = (jnp.arange(NCB, dtype=jnp.int32)[:, None] == tile_cols[None, :]).astype(
        jnp.float32
    )
    return jnp.dot(column_hot, product, precision=lax.Precision.HIGHEST).reshape(-1)


def per_device(
    matrix_tiles,
    tile_column,
    block_counts,
    destination,
    row_bounds,
    dual_start,
    primal_start,
    cost_vector,
    upper_bound,
):
    blocks = block_counts.shape[0]
    rows_per = matrix_tiles.shape[1]
    slot_count = matrix_tiles.shape[0]
    starts = jnp.cumsum(block_counts) - block_counts
    slot_ids = jnp.arange(slot_count, dtype=jnp.int32)
    owners = jnp.sum((starts[None, 1:] <= slot_ids[:, None]).astype(jnp.int32), axis=1)
    bounds_here = row_bounds.reshape(blocks, rows_per)
    dual_here = dual_start.reshape(blocks, rows_per)
    peer_ids = jnp.arange(blocks, dtype=jnp.int32)
    inverse = jnp.sum(
        jnp.where(destination[None, :] == peer_ids[:, None], peer_ids[None, :], 0), axis=1
    )
    tile_store = (matrix_tiles, tile_column, owners, slot_ids < jnp.sum(block_counts))
    bounds = bounds_here.astype(jnp.float32)
    dual_state = dual_here.astype(jnp.float32)
    primal = primal_start
    weight = jnp.ones((), jnp.float32)
    row_image = row_products(tile_store, primal.astype(jnp.bfloat16), blocks)
    for iteration in range(ITERS):
        step_primal = step_scale / weight
        step_dual = step_scale * weight
        partial_value = column_products(tile_store, dual_state.astype(jnp.bfloat16))
        gradient = lax.psum(partial_value, ("grp", "dev"))
        primal_next = jnp.clip(primal - step_primal * (cost_vector - gradient), 0.0, upper_bound)
        change = jnp.sum((primal_next - primal) ** 2)
        next_image = row_products(tile_store, primal_next.astype(jnp.bfloat16), blocks)
        dual_state = jnp.maximum(
            dual_state + step_dual * (bounds - (2.0 * next_image - row_image)), 0.0
        )
        violation_part = jnp.sum(jnp.maximum(bounds - next_image, 0.0) ** 2)
        violation = lax.psum(violation_part, ("grp", "dev"))
        weight = jnp.sqrt(weight * jnp.sqrt((violation + 1e-06) / (change + 1e-06)))
        primal = primal_next
        row_image = next_image
    dual_final = lax.all_to_all(
        dual_state[inverse], "dev", split_axis=0, concat_axis=0, tiled=True
    ).reshape(-1)
    return (primal, dual_final, jnp.reshape(weight, (1,)))


def solution(mesh):
    in_specs = (
        P(("grp", "dev"), None, None),
        P(("grp", "dev")),
        P(("grp", "dev")),
        P(("grp", "dev")),
        P(("grp", "dev")),
        P(("grp", "dev")),
        P(),
        P(),
        P(),
    )
    out_specs = (P(), P(("grp", "dev")), P())
    return jax.shard_map(
        per_device, mesh=mesh, in_specs=in_specs, out_specs=out_specs, check_vma=False
    )
```

profile of v0, /device:TPU:0, one launch (start us, length us, event | category | flops | bytes accessed | tf_op | source)
XLA Modules:
  0.0 506.8 jit_solution(13658657499883403431)
XLA Ops:
  7.2 1.0 reduce-window.9
  8.2 1.3 fusion.92
  9.7 0.6 iota_compare_fusion.20
  10.3 0.9 fusion.4
  11.2 3.3 fusion.46
  14.5 0.6 convolution_bitcast_fusion.2
  15.1 1.2 copy.28
  16.3 133.6 %all-reduce.4.cloned.1.call-done = f32[262144]{0:T(1024)} async-done(((f32[262144]{0:T(1024)}), f32[262144]{0:T(1024)}) %all-reduce.4.cloned.1.call-update) | async-done | bytes 1048592 | tf_op jit(solution)/shard_map/psum | solution.py:78
  149.9 3.5 multiply_reduce_fusion.2
  153.5 1.0 reshape.95
  154.6 1.3 fusion
  155.8 4.0 fusion.20
  160.2 3.9 fusion.18
  164.2 0.8 fusion.61
  165.4 3.3 fusion.44
  169.3 1.2 copy.29
  170.6 39.6 %psum.43 = f32[]{:T(128)} all-reduce(f32[]{:T(128)} %get-tuple-element.14), channel_id=1, replica_groups=mesh['grp'=4,'dev'=8] {'grp','dev'}, use_global_device_ids=true, to_apply=%region_5.6 | all-reduce | flops 1 | bytes 8 | tf_op jit(solution)/shard_map/psum | solution.py:86
  211.7 88.9 %all-reduce.6.cloned.1.call-done = f32[262144]{0:T(1024)} async-done(((f32[262144]{0:T(1024)}), f32[262144]{0:T(1024)}) %all-reduce.6.cloned.1.call-update) | async-done | bytes 1048592 | tf_op jit(solution)/shard_map/psum | solution.py:78
  300.6 2.4 multiply_reduce_fusion.1
  303.5 3.9 fusion.16
  307.4 0.8 fusion.64
  308.4 3.3 fusion.42
  312.4 1.2 copy.30
  313.7 39.9 %psum.45 = f32[]{:T(128)} all-reduce(f32[]{:T(128)} %get-tuple-element.16), channel_id=1, replica_groups=mesh['grp'=4,'dev'=8] {'grp','dev'}, use_global_device_ids=true, to_apply=%region_9.10 | all-reduce | flops 1 | bytes 8 | tf_op jit(solution)/shard_map/psum | solution.py:86
  355.0 88.6 %all-reduce.8.cloned.1.call-done = f32[262144]{0:T(1024)} async-done(((f32[262144]{0:T(1024)}), f32[262144]{0:T(1024)}) %all-reduce.8.cloned.1.call-update) | async-done | bytes 1048592 | tf_op jit(solution)/shard_map/psum | solution.py:78
  443.6 2.1 multiply_reduce_fusion
  445.7 1.0 copy-done.3
  447.2 3.9 fusion.14
  451.1 0.9 fusion.73
  452.0 1.1 gather_fusion
  453.2 3.6 all-to-all-start
  456.7 40.5 %psum.47 = f32[]{:T(128)} all-reduce(f32[]{:T(128)} %get-tuple-element.10), channel_id=1, replica_groups=mesh['grp'=4,'dev'=8] {'grp','dev'}, use_global_device_ids=true, to_apply=%region_14.15 | all-reduce | flops 1 | bytes 8 | tf_op jit(solution)/shard_map/psum | solution.py:86
  (44 shorter events, 4.4 us)
Async XLA Ops:
  7.2 7.3 %copy-start.5 = (s32[20]{0:T(128)S(1)}, s32[20]{0:T(128)}, u32[]{:S(2)}) copy-start(s32[20]{0:T(128)} %param.10) | copy-start | bytes 244
  7.2 142.8 %copy-start.1 = (f32[262144]{0:T(1024)S(1)}, f32[262144]{0:T(1024)}, u32[]{:S(2)}) copy-start(f32[262144]{0:T(1024)} %param.16) | copy-start | bytes 3145732
  7.2 142.8 %copy-start = (f32[262144]{0:T(1024)S(1)}, f32[262144]{0:T(1024)}, u32[]{:S(2)}) copy-start(f32[262144]{0:T(1024)} %param.17) | copy-start | bytes 3145732
  7.2 142.7 %all-reduce.4.cloned.1.call-start = ((), (), s32[]{:S(2)}) async-start(), calls=%async_computation.1 | async-start | bytes 2097152 | tf_op jit(solution)/shard_map/psum | solution.py:78
  16.3 284.3 %all-reduce.6.cloned.1.call-start = ((), (), s32[]{:S(2)}) async-start(), calls=%async_computation.2 | async-start | bytes 2097152 | tf_op jit(solution)/shard_map/psum | solution.py:78
  153.5 6.3 %copy-start.4 = (bf16[262144]{0:T(1024)(128)(2,1)S(1)}, bf16[262144]{0:T(1024)(128)(2,1)}, u32[]{:S(2)}) copy-start(bf16[262144]{0:T(1024)(128)(2,1)} %get-tuple-element.9) | copy-start | bytes 1572868
  155.8 8.4 %copy-start.7 = (bf16[1024]{0:T(1024)(128)(2,1)S(1)}, bf16[1024]{0:T(1024)(128)(2,1)}, u32[]{:S(2)}) copy-start(bf16[1024]{0:T(1024)(128)(2,1)} %param.13) | copy-start | bytes 6148
  155.8 9.2 %copy-start.6 = (bf16[1024]{0:T(1024)(128)(2,1)S(1)}, bf16[1024]{0:T(1024)(128)(2,1)}, u32[]{:S(2)}) copy-start(bf16[1024]{0:T(1024)(128)(2,1)} %param.14) | copy-start | bytes 6148
  170.5 273.1 %all-reduce.8.cloned.1.call-start = ((), (), s32[]{:S(2)}) async-start(), calls=%async_computation.3 | async-start | bytes 2097152 | tf_op jit(solution)/shard_map/psum | solution.py:78
  307.4 6.1 %copy-start.8 = (s32[8]{0:T(128)S(1)}, s32[8]{0:T(128)}, u32[]{:S(2)}) copy-start(s32[8]{0:T(128)} %param.12) | copy-start | bytes 100
  307.4 136.2 %copy-start.2 = (f32[262144]{0:T(1024)S(1)}, f32[262144]{0:T(1024)}, u32[]{:S(2)}) copy-start(f32[262144]{0:T(1024)} %param.16) | copy-start | bytes 3145732
  445.7 1.0 copy-start.3
  453.2 45.4 %all-to-all-start = ((f32[8,1,128]{2,1,0:T(1,128)}), f32[8,1,128]{2,1,0:T(1,128)S(1)}, u32[]{:S(2)}, u32[]{:S(2)}) async-start(f32[8,1,128]{2,1,0:T(1,128)} %bitcast.22), calls=%async_computation | async-start | bytes 8192 | tf_op jit(solution)/shard_map/all_to_all | solution.py:90
Sparse Core Ops, SparseCore 0:
  16.4 133.4 all-reduce.3
  170.6 129.8 all-reduce.5
  313.7 129.8 all-reduce.7
where the time goes:
time: 508 us; the launch traced here: 507 us
  waiting for transfers between devices  311 us (61%)
  blocking collectives  120 us (24%)
  matrix products  33.4 us (7%)
  between operations  19.3 us (4%)
  other arithmetic  11.3 us (2%)
  local copies, waits for them, and re-layouts  8.01 us (2%)
    psum x3, waiting for transfers between devices, per_device(): gradient = lax.psum(partial_value, ('grp', 'dev'))  311 us
    psum x3, blocking collectives, per_device(): violation = lax.psum(violation_part, ('grp', 'dev'))  120 us
    dot_general x4, matrix products, row_products(): jnp.einsum('src,sc->sr', tile_set, picked, preferred_element_type=jnp.flo...  15.8 us
  transfers between devices with their start and end apart: 4, of which 3 were waited for; matrix products, arithmetic and copies ran while one was open for 0% of the time, Pallas kernels for 0%

commit v1 on v0

--- a/solution.py
+++ b/solution.py
@@ -75,7 +75,7 @@
         step_primal = step_scale / weight
         step_dual = step_scale * weight
         partial_value = column_products(tile_store, dual_state.astype(jnp.bfloat16))
-        gradient = lax.psum(partial_value, ("grp", "dev"))
+        gradient = jnp.sum(lax.all_gather(partial_value, ("grp", "dev")), axis=0)
         primal_next = jnp.clip(primal - step_primal * (cost_vector - gradient), 0.0, upper_bound)
         change = jnp.sum((primal_next - primal) ** 2)
         next_image = row_products(tile_store, primal_next.astype(jnp.bfloat16), blocks)

time: 508 us -> 771 us (1.52)
  waiting for transfers between devices: 311 us -> 498 us
  other arithmetic: 11.3 us -> 81.1 us
    all_gather x0 -> x3, waiting for transfers between devices: none -> 498 us  [per_device(): gradient = jnp.sum(lax.all_gather(partial_value, ('grp', 'dev')), axis=0)]
    psum x3 -> x0, waiting for transfers between devices: 311 us -> none  [per_device(): gradient = lax.psum(partial_value, ('grp', 'dev'))]
    reduce_sum x0 -> x3, other arithmetic: none -> 69.8 us  [per_device(): gradient = jnp.sum(lax.all_gather(partial_value, ('grp', 'dev')), axis=0)]
where the time goes in v1:
time: 771 us; the launch traced here: 770 us
  waiting for transfers between devices  498 us (65%)
  blocking collectives  123 us (16%)
  other arithmetic  81.1 us (11%)
  matrix products  33.4 us (4%)
  between operations  19.3 us (3%)
  local copies, waits for them, and re-layouts  11.2 us (1%)
    all_gather x3, waiting for transfers between devices, per_device(): gradient = jnp.sum(lax.all_gather(partial_value, ('grp', 'dev')), axis=0)  498 us
    psum x3, blocking collectives, per_device(): violation = lax.psum(violation_part, ('grp', 'dev'))  123 us
    reduce_sum x3, other arithmetic, per_device(): gradient = jnp.sum(lax.all_gather(partial_value, ('grp', 'dev')), axis=0)  69.8 us
    dot_general x4, matrix products, row_products(): jnp.einsum('src,sc->sr', tile_set, picked, preferred_element_type=jnp.flo...  15.8 us
  transfers between devices with their start and end apart: 4, of which 3 were waited for; matrix products, arithmetic and copies ran while one was open for 0% of the time, Pallas kernels for 0%

profile of v1, /device:TPU:0, one launch (start us, length us, event | category | flops | bytes accessed | tf_op | source)
XLA Modules:
  0.0 769.7 jit_solution(8297906791132501262)
XLA Ops:
  7.2 0.8 reduce-window.9
  8.1 1.3 fusion.95
  10.2 0.9 fusion.4
  11.0 3.3 fusion.49
  15.0 2.2 reshape.100
  17.3 197.0 %all-gather.7.cloned.1.call-done = f32[32,1,262144]{2,1,0:T(1,128)} async-done(((f32[1,1,262144]{2,1,0:T(1,128)}), f32[32,1,262144]{2,1,0:T(1,128)}) %all-gather.7.cloned.1.call-update) | async-done | bytes 33554448 | tf_op jit(solution)/shard_map/all_gather | solution.py:78
  214.2 23.3 %reduce_sum.112 = f32[262144]{0:T(1024)} reduce(f32[32,1,262144]{2,1,0:T(1,128)} %all-gather.7.cloned.1.call-done, f32[]{:T(128)} %constant.6.clone.1), dimensions={0,1}, to_apply=%region_3.4 | reduce | flops 8126464 | bytes 34603012 | tf_op jit(solution)/shard_map/reduce_sum | solution.py:78
  237.5 3.6 multiply_reduce_fusion.2
  241.2 1.0 reshape.85
  242.2 1.3 fusion
  243.5 4.0 fusion.23
  247.9 3.9 fusion.21
  251.8 0.8 fusion.64
  253.0 3.3 fusion.47
  257.0 2.2 reshape.102
  259.3 41.6 %psum.21 = f32[]{:T(128)} all-reduce(f32[]{:T(128)} %get-tuple-element.14), channel_id=1, replica_groups=mesh['grp'=4,'dev'=8] {'grp','dev'}, use_global_device_ids=true, to_apply=%region_5.6 | all-reduce | flops 1 | bytes 8 | tf_op jit(solution)/shard_map/psum | solution.py:86
  302.4 150.6 %all-gather.9.cloned.1.call-done = f32[32,1,262144]{2,1,0:T(1,128)} async-done(((f32[1,1,262144]{2,1,0:T(1,128)}), f32[32,1,262144]{2,1,0:T(1,128)}) %all-gather.9.cloned.1.call-update) | async-done | bytes 33554448 | tf_op jit(solution)/shard_map/all_gather | solution.py:78
  453.0 23.3 %reduce_sum.115 = f32[262144]{0:T(1024)} reduce(f32[32,1,262144]{2,1,0:T(1,128)} %all-gather.9.cloned.1.call-done, f32[]{:T(128)} %constant.6.clone.1), dimensions={0,1}, to_apply=%region_7.8 | reduce | flops 8126464 | bytes 34603012 | tf_op jit(solution)/shard_map/reduce_sum | solution.py:78
  476.2 2.4 multiply_reduce_fusion.1
  479.1 3.9 fusion.19
  484.1 3.3 fusion.45
  488.0 2.2 reshape.104
  490.4 41.3 %psum.22 = f32[]{:T(128)} all-reduce(f32[]{:T(128)} %get-tuple-element.16), channel_id=1, replica_groups=mesh['grp'=4,'dev'=8] {'grp','dev'}, use_global_device_ids=true, to_apply=%region_9.10 | all-reduce | flops 1 | bytes 8 | tf_op jit(solution)/shard_map/psum | solution.py:86
  533.2 150.8 %all-gather.11.cloned.1.call-done = f32[32,1,262144]{2,1,0:T(1,128)} async-done(((f32[1,1,262144]{2,1,0:T(1,128)}), f32[32,1,262144]{2,1,0:T(1,128)}) %all-gather.11.cloned.1.call-update) | async-done | bytes 33554448 | tf_op jit(solution)/shard_map/all_gather | solution.py:78
  684.0 23.3 %reduce_sum.118 = f32[262144]{0:T(1024)} reduce(f32[32,1,262144]{2,1,0:T(1,128)} %all-gather.11.cloned.1.call-done, f32[]{:T(128)} %constant.6.clone.1), dimensions={0,1}, to_apply=%region_11.12 | reduce | flops 8126464 | bytes 34603012 | tf_op jit(solution)/shard_map/reduce_sum | solution.py:78
  707.2 2.1 multiply_reduce_fusion
  709.3 1.0 copy-done.3
  710.8 3.9 fusion.17
  714.8 0.9 fusion.76
  715.7 1.1 gather_fusion
  716.8 3.3 all-to-all-start
  720.1 40.0 %psum.23 = f32[]{:T(128)} all-reduce(f32[]{:T(128)} %get-tuple-element.10), channel_id=1, replica_groups=mesh['grp'=4,'dev'=8] {'grp','dev'}, use_global_device_ids=true, to_apply=%region_14.15 | all-reduce | flops 1 | bytes 8 | tf_op jit(solution)/shard_map/psum | solution.py:86
  (47 shorter events, 6.5 us)
Async XLA Ops:
  7.2 7.1 copy-start.5
  7.2 207.1 %all-gather.7.cloned.1.call-start = ((), (), s32[]{:S(2)}) async-start(), calls=%async_computation.1 | async-start | bytes 34603008 | tf_op jit(solution)/shard_map/all_gather | solution.py:78
  17.2 220.3 %copy-start = (f32[262144]{0:T(1024)S(1)}, f32[262144]{0:T(1024)}, u32[]{:S(2)}) copy-start(f32[262144]{0:T(1024)} %param.17) | copy-start | bytes 3145732
  17.2 220.3 %copy-start.1 = (f32[262144]{0:T(1024)S(1)}, f32[262144]{0:T(1024)}, u32[]{:S(2)}) copy-start(f32[262144]{0:T(1024)} %param.16) | copy-start | bytes 3145732
  17.2 435.7 %all-gather.9.cloned.1.call-start = ((), (), s32[]{:S(2)}) async-start(), calls=%async_computation.2 | async-start | bytes 34603008 | tf_op jit(solution)/shard_map/all_gather | solution.py:78
  241.1 6.3 copy-start.4
  243.4 8.4 %copy-start.7 = (bf16[1024]{0:T(1024)(128)(2,1)S(1)}, bf16[1024]{0:T(1024)(128)(2,1)}, u32[]{:S(2)}) copy-start(bf16[1024]{0:T(1024)(128)(2,1)} %param.13) | copy-start | bytes 6148
  243.4 9.2 %copy-start.6 = (bf16[1024]{0:T(1024)(128)(2,1)S(1)}, bf16[1024]{0:T(1024)(128)(2,1)}, u32[]{:S(2)}) copy-start(bf16[1024]{0:T(1024)(128)(2,1)} %param.14) | copy-start | bytes 6148
  259.2 424.8 %all-gather.11.cloned.1.call-start = ((), (), s32[]{:S(2)}) async-start(), calls=%async_computation.3 | async-start | bytes 34603008 | tf_op jit(solution)/shard_map/all_gather | solution.py:78
  483.1 7.2 copy-start.8
  533.2 174.0 %copy-start.2 = (f32[262144]{0:T(1024)S(1)}, f32[262144]{0:T(1024)}, u32[]{:S(2)}) copy-start(f32[262144]{0:T(1024)} %param.16) | copy-start | bytes 3145732
  709.3 1.0 copy-start.3
  716.8 44.6 %all-to-all-start = ((f32[8,1,128]{2,1,0:T(1,128)}), f32[8,1,128]{2,1,0:T(1,128)S(1)}, u32[]{:S(2)}, u32[]{:S(2)}) async-start(f32[8,1,128]{2,1,0:T(1,128)} %bitcast.22), calls=%async_computation | async-start | bytes 8192 | tf_op jit(solution)/shard_map/all_to_all | solution.py:90
Sparse Core Ops, SparseCore 0:
  17.3 196.8 all-gather.6
  259.3 193.5 all-gather.8
  490.4 193.5 all-gather.10
